TPU v7x, 256 devices: a whole 4x4x8 slice. The times are simulated.
256 devices in a mesh: blk: 8 (over x, core), uly: 32 (over z, y).
Axes of the slice: x: 4, y: 4, z: 8, core: 2. Of those that a mesh axis runs over, the one named last changes fastest.
Arguments:
- query: bfloat16 [32768, 4096], P(('blk', 'uly')), may hold values from -5 to 5
- key_input: bfloat16 [32768, 512], P(('blk', 'uly')), may hold values from -5 to 5
- value_input: bfloat16 [32768, 512], P(('blk', 'uly')), may hold values from -6 to 6
- output: bfloat16 [32768, 4096], P(('blk', 'uly')), may hold values from -6 to 6
- out_grad: bfloat16 [32768, 4096], P(('blk', 'uly')), may hold values from -6 to 6
Outputs:
- query_grad: bfloat16 [32768, 4096], P(('blk', 'uly'))
- key_gradient: bfloat16 [32768, 512], P(('blk', 'uly'))
- value_gradient: bfloat16 [32768, 512], P(('blk', 'uly'))
All inputs are finite; a program needn't handle non-finite values.
Results may differ from a plain program's by a relative error of at most 0.009.
Values may be sent and summed in bfloat16 or wider, within the bound.
A program may use at most 64 MiB of HBM per device.

v0:
```python
import jax
import jax.numpy as jnp
from jax import lax
from jax.sharding import PartitionSpec as P

QUERY_HEADS = 32
KEY_VALUE_HEADS = 4
HEAD_SIZE = 128
WINDOW_KEYS = 1024


def shifted(value, axis, steps):
    count = lax.axis_size(axis)
    leading, last = (max(0, -steps), min(count, count - steps))
    return lax.ppermute(value, axis, [(source, source + steps) for source in range(leading, last)])


def local(query, key_input, value_input, output, out_grad):
    token_rows = query.shape[0]
    ulysses_count = lax.axis_size("uly")
    local_heads = QUERY_HEADS // ulysses_count
    group_extent = ulysses_count // KEY_VALUE_HEADS
    scaling = HEAD_SIZE ** (-0.5)
    rows_here = token_rows * ulysses_count
    block = min(512, rows_here)
    span = WINDOW_KEYS + block
    block_count = rows_here // block
    own_dot = jnp.sum(
        output.reshape(token_rows, QUERY_HEADS, HEAD_SIZE).astype(jnp.float32)
        * out_grad.reshape(token_rows, QUERY_HEADS, HEAD_SIZE).astype(jnp.float32),
        axis=2,
    )
    query_here, grad_here = (
        lax.all_to_all(query, "uly", split_axis=1, concat_axis=0, tiled=True),
        lax.all_to_all(out_grad, "uly", split_axis=1, concat_axis=0, tiled=True),
    )
    row_dot = lax.all_to_all(own_dot, "uly", split_axis=1, concat_axis=0, tiled=True)

    def repeat_groups(value_entries):
        return jnp.repeat(
            value_entries.reshape(token_rows, KEY_VALUE_HEADS, HEAD_SIZE), group_extent, axis=1
        ).reshape(token_rows, ulysses_count * HEAD_SIZE)

    key_head, value_head = (
        lax.all_to_all(repeat_groups(key_input), "uly", split_axis=1, concat_axis=0, tiled=True),
        lax.all_to_all(repeat_groups(value_input), "uly", split_axis=1, concat_axis=0, tiled=True),
    )
    queries = query_here.reshape(rows_here, local_heads, HEAD_SIZE)
    grads_out = grad_here.reshape(rows_here, local_heads, HEAD_SIZE)
    tail_keys, tail_values = shifted(
        (key_head[rows_here - WINDOW_KEYS :], value_head[rows_here - WINDOW_KEYS :]), "blk", 1
    )
    key_ext = jnp.concatenate([tail_keys, key_head], axis=0)
    value_ext = jnp.concatenate([tail_values, value_head], axis=0)
    block_anchor = lax.axis_index("blk") * rows_here - WINDOW_KEYS
    offsets = jnp.arange(block, dtype=jnp.int32)[:, None]
    columns = jnp.arange(span, dtype=jnp.int32)[None, :]
    relative = columns - offsets
    inside = (relative >= 1) & (relative <= WINDOW_KEYS)

    def block_step(index, carry):
        query_acc, key_acc, value_acc = carry
        start = index * block
        query_block = lax.dynamic_slice_in_dim(queries, start, block, 0)
        grad_block = lax.dynamic_slice_in_dim(grads_out, start, block, 0)
        dot_block = lax.dynamic_slice_in_dim(row_dot, start, block, 0)
        key_block = lax.dynamic_slice_in_dim(key_ext, start, span, 0)
        value_block = lax.dynamic_slice_in_dim(value_ext, start, span, 0)
        visible = (inside & (block_anchor + start + columns >= 0))[None, :, :]
        scores = (
            jnp.einsum("qhd,kd->hqk", query_block, key_block, preferred_element_type=jnp.float32)
            * scaling
        )
        masked = jnp.where(visible, scores, -1e30)
        row_max = jnp.max(masked, axis=2)
        row_sum = jnp.sum(jnp.where(visible, jnp.exp(masked - row_max[:, :, None]), 0.0), axis=2)
        log_total = row_max + jnp.log(row_sum)
        weights = jnp.where(visible, jnp.exp(masked - log_total[:, :, None]), 0.0)
        weights_low = weights.astype(jnp.bfloat16)
        weight_grad = jnp.einsum(
            "qhd,kd->hqk", grad_block, value_block, preferred_element_type=jnp.float32
        )
        score_grad = (weights * (weight_grad - dot_block.T[:, :, None]) * scaling).astype(
            jnp.bfloat16
        )
        query_portion = jnp.einsum(
            "hqk,kd->qhd", score_grad, key_block, preferred_element_type=jnp.float32
        )
        key_portion = jnp.einsum(
            "hqk,qhd->kd", score_grad, query_block, preferred_element_type=jnp.float32
        )
        value_portion = jnp.einsum(
            "hqk,qhd->kd", weights_low, grad_block, preferred_element_type=jnp.float32
        )
        query_acc = lax.dynamic_update_slice_in_dim(query_acc, query_portion, start, 0)
        key_acc = lax.dynamic_update_slice_in_dim(
            key_acc, lax.dynamic_slice_in_dim(key_acc, start, span, 0) + key_portion, start, 0
        )
        value_acc = lax.dynamic_update_slice_in_dim(
            value_acc, lax.dynamic_slice_in_dim(value_acc, start, span, 0) + value_portion, start, 0
        )
        return (query_acc, key_acc, value_acc)

    grad_init = (
        jnp.zeros((rows_here, local_heads, HEAD_SIZE), jnp.float32),
        jnp.zeros((WINDOW_KEYS + rows_here, HEAD_SIZE), jnp.float32),
        jnp.zeros((WINDOW_KEYS + rows_here, HEAD_SIZE), jnp.float32),
    )
    query_acc, key_acc, value_acc = lax.fori_loop(0, block_count, block_step, grad_init)
    tail_key, tail_value = (
        shifted(key_acc[:WINDOW_KEYS].astype(jnp.bfloat16), "blk", -1).astype(jnp.float32),
        shifted(value_acc[:WINDOW_KEYS].astype(jnp.bfloat16), "blk", -1).astype(jnp.float32),
    )
    key_own = jnp.concatenate(
        [key_acc[WINDOW_KEYS:rows_here], key_acc[rows_here:] + tail_key], axis=0
    )
    value_own = jnp.concatenate(
        [value_acc[WINDOW_KEYS:rows_here], value_acc[rows_here:] + tail_value], axis=0
    )
    query_low = query_acc.astype(jnp.bfloat16).reshape(rows_here, local_heads * HEAD_SIZE)
    query_grad = lax.all_to_all(query_low, "uly", split_axis=0, concat_axis=1, tiled=True)
    key_portions, value_portions = (
        lax.all_to_all(
            key_own.reshape(ulysses_count, token_rows, HEAD_SIZE).astype(jnp.bfloat16),
            "uly",
            split_axis=0,
            concat_axis=0,
            tiled=True,
        ).astype(jnp.float32),
        lax.all_to_all(
            value_own.reshape(ulysses_count, token_rows, HEAD_SIZE).astype(jnp.bfloat16),
            "uly",
            split_axis=0,
            concat_axis=0,
            tiled=True,
        ).astype(jnp.float32),
    )
    key_totals = key_portions.reshape(KEY_VALUE_HEADS, group_extent, token_rows, HEAD_SIZE).sum(
        axis=1
    )
    value_totals = value_portions.reshape(KEY_VALUE_HEADS, group_extent, token_rows, HEAD_SIZE).sum(
        axis=1
    )
    key_gradient = (
        key_totals.transpose(1, 0, 2)
        .reshape(token_rows, KEY_VALUE_HEADS * HEAD_SIZE)
        .astype(jnp.bfloat16)
    )
    value_gradient = (
        value_totals.transpose(1, 0, 2)
        .reshape(token_rows, KEY_VALUE_HEADS * HEAD_SIZE)
        .astype(jnp.bfloat16)
    )
    return (query_grad, key_gradient, value_gradient)


def solution(mesh):
    in_specs = (
        P(("blk", "uly"), None),
        P(("blk", "uly"), None),
        P(("blk", "uly"), None),
        P(("blk", "uly"), None),
        P(("blk", "uly"), None),
    )
    out_specs = (P(("blk", "uly"), None), P(("blk", "uly"), None), P(("blk", "uly"), None))
    return jax.shard_map(local, mesh=mesh, in_specs=in_specs, out_specs=out_specs, check_vma=False)
```

profile of v0, /device:TPU:6, one launch (start us, length us, event | category | flops | bytes accessed | tf_op | source)
XLA Modules:
  0.0 363.4 jit_solution(16737507312744375295)
XLA Ops:
  2.8 11.5 %all-to-all-start = ((bf16[128,32,128]{2,0,1:T(8,128)(2,1)}), bf16[128,32,128]{2,0,1:T(8,128)(2,1)S(1)}, u32[]{:S(2)}, u32[]{:S(2)}) async-start(bf16[128,32,128]{2,0,1:T(8,128)(2,1)} %bitcast), calls=%async_computation | async-start | bytes 2097152 | tf_op jit(solution)/shard_map/all_to_all | solution.py:45
  14.3 28.0 %all-to-all-done = bf16[128,32,128]{2,0,1:T(8,128)(2,1)S(1)} async-done(((bf16[128,32,128]{2,0,1:T(8,128)(2,1)}), bf16[128,32,128]{2,0,1:T(8,128)(2,1)S(1)}, u32[]{:S(2)}, u32[]{:S(2)}) %all-to-all-start) | async-done | bytes 1048608 | tf_op jit(solution)/shard_map/all_to_all | solution.py:45
  43.5 5.6 %all-to-all-start.2 = ((bf16[128,32,128]{2,0,1:T(8,128)(2,1)}), bf16[128,32,128]{2,0,1:T(8,128)(2,1)S(1)}, u32[]{:S(2)}, u32[]{:S(2)}) async-start(bf16[128,32,128]{2,0,1:T(8,128)(2,1)} %bitcast.154), calls=%async_computation.2 | async-start | bytes 2097152 | tf_op jit(solution)/shard_map/all_to_all | solution.py:46
  49.1 2.3 copy.36
  51.4 24.7 %all-to-all-done.2 = bf16[128,32,128]{2,0,1:T(8,128)(2,1)S(1)} async-done(((bf16[128,32,128]{2,0,1:T(8,128)(2,1)}), bf16[128,32,128]{2,0,1:T(8,128)(2,1)S(1)}, u32[]{:S(2)}, u32[]{:S(2)}) %all-to-all-start.2) | async-done | bytes 1048608 | tf_op jit(solution)/shard_map/all_to_all | solution.py:46
  76.1 5.7 %all-to-all-start.3 = ((bf16[128,32,128]{0,2,1:T(8,128)(2,1)}), bf16[128,32,128]{0,2,1:T(8,128)(2,1)}, u32[]{:S(2)}, u32[]{:S(2)}) async-start(bf16[128,32,128]{0,2,1:T(8,128)(2,1)} %bitcast.11), calls=%async_computation.3 | async-start | bytes 2097152 | tf_op jit(solution)/shard_map/all_to_all | solution.py:35
  81.8 2.3 copy.33
  84.1 24.3 %all-to-all-done.3 = bf16[128,32,128]{0,2,1:T(8,128)(2,1)} async-done(((bf16[128,32,128]{0,2,1:T(8,128)(2,1)}), bf16[128,32,128]{0,2,1:T(8,128)(2,1)}, u32[]{:S(2)}, u32[]{:S(2)}) %all-to-all-start.3) | async-done | bytes 1048608 | tf_op jit(solution)/shard_map/all_to_all | solution.py:35
  108.4 5.7 %all-to-all-start.1 = ((bf16[128,32,128]{0,2,1:T(8,128)(2,1)}), bf16[128,32,128]{0,2,1:T(8,128)(2,1)}, u32[]{:S(2)}, u32[]{:S(2)}) async-start(bf16[128,32,128]{0,2,1:T(8,128)(2,1)} %bitcast.151), calls=%async_computation.1 | async-start | bytes 2097152 | tf_op jit(solution)/shard_map/all_to_all | solution.py:34
  114.2 1.9 collective-permute-start
  116.1 2.3 copy.38
  118.4 2.5 fusion.45
  120.9 1.9 collective-permute-start.1
  122.8 2.3 copy.37
  125.1 15.5 %all-to-all-done.1 = bf16[128,32,128]{0,2,1:T(8,128)(2,1)} async-done(((bf16[128,32,128]{0,2,1:T(8,128)(2,1)}), bf16[128,32,128]{0,2,1:T(8,128)(2,1)}, u32[]{:S(2)}, u32[]{:S(2)}) %all-to-all-start.1) | async-done | bytes 1048608 | tf_op jit(solution)/shard_map/all_to_all | solution.py:34
  140.6 5.6 %all-to-all-start.4 = ((f32[128,32,1]{0,2,1:T(1,128)}), f32[128,32,1]{0,2,1:T(1,128)S(1)}, u32[]{:S(2)}, u32[]{:S(2)}) async-start(f32[128,32,1]{0,2,1:T(1,128)} %bitcast.15), calls=%async_computation.4 | async-start | bytes 32768 | tf_op jit(solution)/shard_map/all_to_all | solution.py:37
  146.2 2.3 copy.34
  150.7 5.1 %all-to-all-done.4 = f32[128,32,1]{0,2,1:T(1,128)S(1)} async-done(((f32[128,32,1]{0,2,1:T(1,128)}), f32[128,32,1]{0,2,1:T(1,128)S(1)}, u32[]{:S(2)}, u32[]{:S(2)}) %all-to-all-start.4) | async-done | bytes 16416 | tf_op jit(solution)/shard_map/all_to_all | solution.py:37
  158.8 108.1 %while.18 = (s32[]{:T(128)}, bf16[4096,1,128]{0,2,1:T(8,128)(2,1)}, f32[5120,128]{1,0:T(8,128)S(1)}, f32[5120,128]{1,0:T(8,128)}, bf16[5120,128]{1,0:T(8,128)(2,...) while((s32[]{:T(128)}, bf16[4096,1,128]{0,2,1:T(8,128)(2,1)}, ...), condition=%wide.region_4.5_spmd.clone, body=%wide.region_1.4_spmd.clone.sunk | while | flops 1034553856 | bytes 22443792 | solution.py:109
  158.8 2.5 fusion.72
  161.4 1.8 select_reduce_fusion.2
  163.2 3.5 fusion.76
  166.7 2.0 fusion.73
  170.3 2.1 fusion.74
  172.4 2.5 fusion.72
  176.7 3.5 fusion.76
  180.2 2.0 fusion.73
  183.8 2.1 fusion.74
  185.9 2.5 fusion.72
  190.2 3.5 fusion.76
  193.7 2.0 fusion.73
  197.3 2.1 fusion.74
  199.4 2.5 fusion.72
  203.7 3.5 fusion.76
  207.2 2.0 fusion.73
  210.8 2.1 fusion.74
  212.9 2.5 fusion.72
  217.2 3.5 fusion.76
  220.7 2.0 fusion.73
  224.3 2.1 fusion.74
  226.4 2.5 fusion.72
  230.7 3.5 fusion.76
  234.2 2.0 fusion.73
  237.8 2.1 fusion.74
  239.9 2.5 fusion.72
  244.2 3.5 fusion.76
  247.8 2.0 fusion.73
  251.3 2.1 fusion.74
  253.4 2.5 fusion.72
  257.8 3.5 fusion.76
  261.3 2.0 fusion.73
  264.8 2.1 fusion.74
  266.9 2.3 copy.39
  269.1 4.8 %all-to-all-start.5 = ((bf16[32,128,128]{2,1,0:T(8,128)(2,1)}), bf16[32,128,128]{2,1,0:T(8,128)(2,1)}, u32[]{:S(2)}, u32[]{:S(2)}) async-start(bf16[32,128,128]{2,1,0:T(8,128)(2,1)} %bitcast.153), calls=%async_computation.5 | async-start | bytes 2097152 | tf_op jit(solution)/shard_map/all_to_all | solution.py:121
  273.9 1.9 convert.21
  275.8 1.9 collective-permute-start.3
  277.8 3.8 %collective-permute-done.3 = bf16[1024,128]{1,0:T(8,128)(2,1)S(1)} collective-permute-done((bf16[1024,128]{1,0:T(8,128)(2,1)S(1)}, bf16[1024,128]{1,0:T(8,128)(2,1)S(1)}, u32[]{:S(2)}, u32[]{:S(2)}) %collective-permute-start.3) | collective-permute-done | bytes 262176 | tf_op jit(solution)/shard_map/ppermute | solution.py:15
  283.8 16.2 %all-to-all-done.5 = bf16[32,128,128]{2,1,0:T(8,128)(2,1)} async-done(((bf16[32,128,128]{2,1,0:T(8,128)(2,1)}), bf16[32,128,128]{2,1,0:T(8,128)(2,1)}, u32[]{:S(2)}, u32[]{:S(2)}) %all-to-all-start.5) | async-done | bytes 1048608 | tf_op jit(solution)/shard_map/all_to_all | solution.py:121
  299.9 5.6 %all-to-all-start.7 = ((bf16[32,128,128]{2,1,0:T(8,128)(2,1)}), bf16[32,128,128]{2,1,0:T(8,128)(2,1)}, u32[]{:S(2)}, u32[]{:S(2)}) async-start(bf16[32,128,128]{2,1,0:T(8,128)(2,1)} %bitcast.152), calls=%async_computation.7 | async-start | bytes 2097152 | tf_op jit(solution)/shard_map/all_to_all | solution.py:130
  305.7 1.9 collective-permute-start.2
  307.7 3.8 %collective-permute-done.2 = bf16[1024,128]{1,0:T(8,128)(2,1)S(1)} collective-permute-done((bf16[1024,128]{1,0:T(8,128)(2,1)S(1)}, bf16[1024,128]{1,0:T(8,128)(2,1)S(1)}, u32[]{:S(2)}, u32[]{:S(2)}) %collective-permute-start.2) | collective-permute-done | bytes 262176 | tf_op jit(solution)/shard_map/ppermute | solution.py:15
  312.7 18.7 %all-to-all-done.7 = bf16[32,128,128]{2,1,0:T(8,128)(2,1)} async-done(((bf16[32,128,128]{2,1,0:T(8,128)(2,1)}), bf16[32,128,128]{2,1,0:T(8,128)(2,1)}, u32[]{:S(2)}, u32[]{:S(2)}) %all-to-all-start.7) | async-done | bytes 1048608 | tf_op jit(solution)/shard_map/all_to_all | solution.py:130
  331.4 5.3 %all-to-all-start.6 = ((bf16[32,128,128]{2,1,0:T(8,128)(2,1)}), bf16[32,128,128]{2,1,0:T(8,128)(2,1)S(1)}, u32[]{:S(2)}, u32[]{:S(2)}) async-start(bf16[32,128,128]{2,1,0:T(8,128)(2,1)} %bitcast.21), calls=%async_computation.6 | async-start | bytes 2097152 | tf_op jit(solution)/shard_map/all_to_all | solution.py:123
  341.9 20.4 %all-to-all-done.6 = bf16[32,128,128]{2,1,0:T(8,128)(2,1)S(1)} async-done(((bf16[32,128,128]{2,1,0:T(8,128)(2,1)}), bf16[32,128,128]{2,1,0:T(8,128)(2,1)S(1)}, u32[]{:S(2)}, u32[]{:S(2)}) %all-to-all-start.6) | async-done | bytes 1048608 | tf_op jit(solution)/shard_map/all_to_all | solution.py:123
  (73 shorter events, 43.6 us)
Async XLA Ops:
  0.6 0.9 copy-start
  0.6 13.6 %copy-start.1 = (bf16[128,512]{1,0:T(8,128)(2,1)S(1)}, bf16[128,512]{1,0:T(8,128)(2,1)}, u32[]{:S(2)}) copy-start(bf16[128,512]{1,0:T(8,128)(2,1)} %param.9) | copy-start | bytes 393220
  2.8 39.5 %all-to-all-start = ((bf16[128,32,128]{2,0,1:T(8,128)(2,1)}), bf16[128,32,128]{2,0,1:T(8,128)(2,1)S(1)}, u32[]{:S(2)}, u32[]{:S(2)}) async-start(bf16[128,32,128]{2,0,1:T(8,128)(2,1)} %bitcast), calls=%async_computation | async-start | bytes 2097152 | tf_op jit(solution)/shard_map/all_to_all | solution.py:45
  43.5 32.6 %all-to-all-start.2 = ((bf16[128,32,128]{2,0,1:T(8,128)(2,1)}), bf16[128,32,128]{2,0,1:T(8,128)(2,1)S(1)}, u32[]{:S(2)}, u32[]{:S(2)}) async-start(bf16[128,32,128]{2,0,1:T(8,128)(2,1)} %bitcast.154), calls=%async_computation.2 | async-start | bytes 2097152 | tf_op jit(solution)/shard_map/all_to_all | solution.py:46
  76.1 32.3 %all-to-all-start.3 = ((bf16[128,32,128]{0,2,1:T(8,128)(2,1)}), bf16[128,32,128]{0,2,1:T(8,128)(2,1)}, u32[]{:S(2)}, u32[]{:S(2)}) async-start(bf16[128,32,128]{0,2,1:T(8,128)(2,1)} %bitcast.11), calls=%async_computation.3 | async-start | bytes 2097152 | tf_op jit(solution)/shard_map/all_to_all | solution.py:35
  108.4 32.2 %all-to-all-start.1 = ((bf16[128,32,128]{0,2,1:T(8,128)(2,1)}), bf16[128,32,128]{0,2,1:T(8,128)(2,1)}, u32[]{:S(2)}, u32[]{:S(2)}) async-start(bf16[128,32,128]{0,2,1:T(8,128)(2,1)} %bitcast.151), calls=%async_computation.1 | async-start | bytes 2097152 | tf_op jit(solution)/shard_map/all_to_all | solution.py:34
  114.2 34.3 %collective-permute-start = (bf16[1024,128]{1,0:T(8,128)(2,1)S(1)}, bf16[1024,128]{1,0:T(8,128)(2,1)S(1)}, u32[]{:S(2)}, u32[]{:S(2)}) collective-permute-start(bf16[1024,128]{1,0:T(8,128)(2,1)S(1)} %bitcast.162), channel_id=1, source_target_pairs={{0,32},{32,64},{64,96},{96,128},{128,160},{160,192},{192,224},{1,3... | collective-permute-start | bytes 786440 | tf_op jit(solution)/shard_map/ppermute | solution.py:15
  120.9 28.7 %collective-permute-start.1 = (bf16[1024,128]{1,0:T(8,128)(2,1)S(1)}, bf16[1024,128]{1,0:T(8,128)(2,1)S(1)}, u32[]{:S(2)}, u32[]{:S(2)}) collective-permute-start(bf16[1024,128]{1,0:T(8,128)(2,1)S(1)} %bitcast.163), channel_id=1, source_target_pairs={{0,32},{32,64},{64,96},{96,128},{128,160},{160,192},{192,224},{1,3... | collective-permute-start | bytes 786440 | tf_op jit(solution)/shard_map/ppermute | solution.py:15
  140.6 15.3 %all-to-all-start.4 = ((f32[128,32,1]{0,2,1:T(1,128)}), f32[128,32,1]{0,2,1:T(1,128)S(1)}, u32[]{:S(2)}, u32[]{:S(2)}) async-start(f32[128,32,1]{0,2,1:T(1,128)} %bitcast.15), calls=%async_computation.4 | async-start | bytes 32768 | tf_op jit(solution)/shard_map/all_to_all | solution.py:37
  269.1 30.8 %all-to-all-start.5 = ((bf16[32,128,128]{2,1,0:T(8,128)(2,1)}), bf16[32,128,128]{2,1,0:T(8,128)(2,1)}, u32[]{:S(2)}, u32[]{:S(2)}) async-start(bf16[32,128,128]{2,1,0:T(8,128)(2,1)} %bitcast.153), calls=%async_computation.5 | async-start | bytes 2097152 | tf_op jit(solution)/shard_map/all_to_all | solution.py:121
  275.8 5.8 %collective-permute-start.3 = (bf16[1024,128]{1,0:T(8,128)(2,1)S(1)}, bf16[1024,128]{1,0:T(8,128)(2,1)S(1)}, u32[]{:S(2)}, u32[]{:S(2)}) collective-permute-start(bf16[1024,128]{1,0:T(8,128)(2,1)S(1)} %slice.49), channel_id=1, source_target_pairs={{32,0},{64,32},{96,64},{128,96},{160,128},{192,160},{224,192},{33,... | collective-permute-start | bytes 786440 | tf_op jit(solution)/shard_map/ppermute | solution.py:15
  299.9 31.5 %all-to-all-start.7 = ((bf16[32,128,128]{2,1,0:T(8,128)(2,1)}), bf16[32,128,128]{2,1,0:T(8,128)(2,1)}, u32[]{:S(2)}, u32[]{:S(2)}) async-start(bf16[32,128,128]{2,1,0:T(8,128)(2,1)} %bitcast.152), calls=%async_computation.7 | async-start | bytes 2097152 | tf_op jit(solution)/shard_map/all_to_all | solution.py:130
  305.7 5.8 %collective-permute-start.2 = (bf16[1024,128]{1,0:T(8,128)(2,1)S(1)}, bf16[1024,128]{1,0:T(8,128)(2,1)S(1)}, u32[]{:S(2)}, u32[]{:S(2)}) collective-permute-start(bf16[1024,128]{1,0:T(8,128)(2,1)S(1)} %slice.47), channel_id=1, source_target_pairs={{32,0},{64,32},{96,64},{128,96},{160,128},{192,160},{224,192},{33,... | collective-permute-start | bytes 786440 | tf_op jit(solution)/shard_map/ppermute | solution.py:15
  331.4 30.9 %all-to-all-start.6 = ((bf16[32,128,128]{2,1,0:T(8,128)(2,1)}), bf16[32,128,128]{2,1,0:T(8,128)(2,1)S(1)}, u32[]{:S(2)}, u32[]{:S(2)}) async-start(bf16[32,128,128]{2,1,0:T(8,128)(2,1)} %bitcast.21), calls=%async_computation.6 | async-start | bytes 2097152 | tf_op jit(solution)/shard_map/all_to_all | solution.py:123
where the time goes:
time: 366 us; the launch traced here: 363 us
  waiting for transfers between devices  160 us (44%)
  matrix products  93.2 us (25%)
  starting transfers between devices  57.5 us (16%)
  other arithmetic  26.3 us (7%)
  local copies, waits for them, and re-layouts  24.9 us (7%)
    dot_general x8, matrix products, block_step(): jnp.einsum('hqk,qhd->kd', weights_low, grad_block, preferred_element_type...  28.2 us
    all_to_all x1, waiting for transfers between devices, local(): lax.all_to_all(repeat_groups(key_input), 'uly', split_axis=1, concat_axis...  28 us
    all_to_all x1, waiting for transfers between devices, local(): lax.all_to_all(repeat_groups(value_input), 'uly', split_axis=1, concat_ax...  24.7 us
    all_to_all x1, waiting for transfers between devices, local(): lax.all_to_all(out_grad, 'uly', split_axis=1, concat_axis=0, tiled=True)  24.3 us
    all_to_all x1, waiting for transfers between devices, local(): lax.all_to_all(key_own.reshape(ulysses_count, token_rows, HEAD_SIZE).asty...  20.4 us
    dot_general x8, matrix products, block_step(): jnp.einsum('qhd,kd->hqk', query_block, key_block, preferred_element_type=...  20.2 us
    all_to_all x1, waiting for transfers between devices, local(): lax.all_to_all(value_own.reshape(ulysses_count, token_rows, HEAD_SIZE).as...  18.7 us
    dot_general x8, matrix products, block_step(): jnp.einsum('hqk,kd->qhd', score_grad, key_block, preferred_element_type=j...  16.5 us
  transfers between devices with their start and end apart: 12, of which 10 were waited for; matrix products, arithmetic and copies ran while one was open for 7% of the time, Pallas kernels for 0%

commit v1 on v0

v1 whole, which is shorter than its diff:
```python
import functools

import jax
import jax.numpy as jnp
from jax import lax
from jax.experimental import pallas as pl
from jax.experimental.pallas import tpu as pltpu
from jax.sharding import PartitionSpec as P

QUERY_HEADS = 32
KEY_VALUE_HEADS = 4
HEAD_SIZE = 128
WINDOW_KEYS = 1024
ROW = 4
GROUP = QUERY_HEADS // KEY_VALUE_HEADS
BLOCK = 128
SLOTS = WINDOW_KEYS // BLOCK + 1
PAIR = 2 * BLOCK
STEPS = GROUP // 2
SPAN = SLOTS * BLOCK
SCALE = HEAD_SIZE**-0.5
LOG2E = 1.4426950408889634
BIG = 1e30
BF, F32 = jnp.bfloat16, jnp.float32
NT = (((1,), (1,)), ((), ()))
MESH = pl.DeviceIdType.MESH


def kernel(
    blocks, uly,
    query, key, value, output, out_grad,
    query_grad, key_gradient, value_gradient,
    q, o, g, kv, kt, s, w, wl, sl, acc, part, send, land, dot, dq, dk, dv,
    load_sem, wide_sem, gs, gr, rs, rr, out_sem,
):
    blk, u = lax.axis_index("blk"), lax.axis_index("uly")
    z_count = uly // ROW
    y, z = u % ROW, u // ROW
    device = blk * uly + u
    row = blk * z_count + z
    rows = blocks * z_count
    at_end = (y + 1) // ROW
    at_start = 1 - (y + ROW - 1) // ROW

    def along_y(step):
        return (blk, z * ROW + (y + step + ROW) % ROW)

    def along_z(step):
        to = (row + step + rows) % rows
        return (to // z_count, (to % z_count) * ROW + y)

    right, left = along_y(1), along_y(-1)
    up1, up2, down1, down2 = along_z(1), along_z(2), along_z(-1), along_z(-2)

    def load_kv(h):
        cols = pl.ds(h * HEAD_SIZE, HEAD_SIZE)
        return (
            pltpu.make_async_copy(key.at[:, cols], kv.at[h, 0, 0:BLOCK, :], load_sem.at[h, 0]),
            pltpu.make_async_copy(value.at[:, cols], kv.at[h, 0, BLOCK : 2 * BLOCK, :], load_sem.at[h, 1]),
        )

    for h in range(KEY_VALUE_HEADS):
        for copy in load_kv(h):
            copy.start()

    @pl.loop(0, QUERY_HEADS)
    def _(n):
        cols = pl.ds(pl.multiple_of(n * HEAD_SIZE, HEAD_SIZE), HEAD_SIZE)
        here = pl.ds(pl.multiple_of(n * BLOCK, BLOCK), BLOCK)
        pltpu.make_async_copy(query.at[:, cols], q.at[here, :], wide_sem.at[0]).start()
        pltpu.make_async_copy(out_grad.at[:, cols], g.at[here, :], wide_sem.at[1]).start()
        pltpu.make_async_copy(output.at[:, cols], o.at[here, :], wide_sem.at[2]).start()

    barrier = pltpu.get_barrier_semaphore()
    for other in (right, left, up1, up2, down1, down2):
        pl.semaphore_signal(barrier, inc=1, device_id=other, device_id_type=MESH)
    pl.semaphore_wait(barrier, 6)

    def gather(h, source, to, other):
        return pltpu.make_async_remote_copy(
            src_ref=kv.at[h, source], dst_ref=kv.at[h, to],
            send_sem=gs.at[h, to], recv_sem=gr.at[h, to],
            device_id=other, device_id_type=MESH,
        )

    def arrived(h, slot):
        gather(h, slot, slot, right).wait_recv()

    def gather_start(h):
        for copy in load_kv(h):
            copy.wait()
        gather(h, 0, 4, up1).start()

        @pl.when(y < ROW - 1)
        def _():
            gather(h, 0, 1, right).start()

        @pl.when(y == 0)
        def _():
            gather(h, 0, 3, left).start()

        gather(h, 0, 8, up2).start()

    def gather_mid(h):
        arrived(h, 4)
        gather(h, 4, 5 - 4 * at_end, right).start()
        gather(h, 4, 3 + 4 * at_start, left).start()
        arrived(h, 8)

        @pl.when(y == ROW - 1)
        def _():
            gather(h, 8, 5, right).start()

        @pl.when(y > 0)
        def _():
            gather(h, 8, 7, left).start()

    def gather_forward(h):
        arrived(h, 1)
        arrived(h, 5)
        gather(h, 1 + 4 * at_end, 2, right).start()
        arrived(h, 3)
        arrived(h, 7)
        gather(h, 7 - 4 * at_start, 6, left).start()

    def gather_done(h):
        arrived(h, 2)
        arrived(h, 6)

    def reduce(h, slot, other):
        return pltpu.make_async_remote_copy(
            src_ref=send.at[h, slot], dst_ref=land.at[h, slot],
            send_sem=rs.at[h, slot], recv_sem=rr.at[h, slot],
            device_id=other, device_id_type=MESH,
        )

    def ready(h, slot):
        send[h, slot] = part[h, slot].astype(BF)

    def take(h, slot, into):
        reduce(h, slot, right).wait_recv()
        part[h, into] = part[h, into] + land[h, slot].astype(F32)

    def reduce_start(h):
        ready(h, 2)
        ready(h, 6)
        ready(h, 5 - 4 * at_end)
        ready(h, 3 + 4 * at_start)
        reduce(h, 2, left).start()
        reduce(h, 6, right).start()
        reduce(h, 5 - 4 * at_end, left).start()
        reduce(h, 3 + 4 * at_start, right).start()

    def reduce_mid(h):
        take(h, 2, 1 + 4 * at_end)
        ready(h, 1 + 4 * at_end)
        take(h, 6, 7 - 4 * at_start)
        ready(h, 7 - 4 * at_start)
        reduce(h, 1 + 4 * at_end, left).start()
        reduce(h, 7 - 4 * at_start, right).start()

    def reduce_column(h):
        take(h, 1, 4 * at_end)
        take(h, 5, 4 + 4 * at_end)
        take(h, 3, 4 - 4 * at_start)
        take(h, 7, 8 - 4 * at_start)
        ready(h, 4)
        ready(h, 8)
        reduce(h, 4, down1).start()
        reduce(h, 8, down2).start()

    def reduce_finish(h):
        take(h, 4, 0)
        take(h, 8, 0)
        cols = pl.ds(pl.multiple_of(h * HEAD_SIZE, HEAD_SIZE), HEAD_SIZE)
        dk[:, cols] = part[h, 0, 0:BLOCK, :].astype(BF)
        dv[:, cols] = part[h, 0, BLOCK : 2 * BLOCK, :].astype(BF)

    lane = lax.broadcasted_iota(jnp.int32, (BLOCK, PAIR), 1) % BLOCK
    mask = lax.broadcasted_iota(jnp.int32, (BLOCK, PAIR), 0) <= lane

    def prepare(h):
        for k in range(SLOTS):
            kt[:, k * BLOCK : (k + 1) * BLOCK] = jnp.transpose(kv[h, k, 0:BLOCK, :])
        acc[...] = jnp.zeros_like(acc)

    def pair(h, n):
        base = pl.multiple_of((h * STEPS + n) * PAIR, PAIR)
        at = pl.ds(base, PAIR)
        qn, gn = q[at, :], g[at, :]
        keys = kv[h, :, 0:BLOCK, :].reshape(SPAN, HEAD_SIZE)
        values = kv[h, :, BLOCK : 2 * BLOCK, :].reshape(SPAN, HEAD_SIZE)
        s[...] = lax.dot_general(keys, qn, NT, preferred_element_type=F32)
        w[...] = lax.dot_general(values, gn, NT, preferred_element_type=F32)
        product = o[at, :].astype(F32) * gn.astype(F32)
        high = product.astype(BF)
        low = (product - high.astype(F32)).astype(BF)
        ones = jnp.ones((8, HEAD_SIZE), BF)
        row_dot = (
            lax.dot_general(ones, high, NT, preferred_element_type=F32)
            + lax.dot_general(ones, low, NT, preferred_element_type=F32)
        )[0:1, :]

        def chunk(k):
            return pl.ds(k * BLOCK, BLOCK)

        def hidden(k):
            return jnp.where(device >= k, 0.0, BIG).astype(F32)

        edge = jnp.where(mask, s[chunk(0), :], s[chunk(8), :] - hidden(8))
        s[chunk(0), :] = edge
        top = jnp.max(edge, axis=0, keepdims=True)
        for k in range(1, SLOTS - 1):
            top = jnp.maximum(top, jnp.max(s[chunk(k), :], axis=0, keepdims=True) - hidden(k))
        factor = SCALE * LOG2E
        total = jnp.zeros((1, PAIR), F32)
        for k in range(SLOTS - 1):
            p = jnp.exp2((s[chunk(k), :] - (top + hidden(k))) * factor)
            s[chunk(k), :] = p
            total = total + jnp.sum(p, axis=0, keepdims=True)
        inverse = 1.0 / total
        weights = s[chunk(0), :] * inverse
        grads = weights * (jnp.where(mask, w[chunk(0), :], w[chunk(8), :]) - row_dot)
        wl[chunk(0), :] = jnp.where(mask, weights, 0.0).astype(BF)
        wl[chunk(8), :] = jnp.where(mask, 0.0, weights).astype(BF)
        sl[chunk(0), :] = jnp.where(mask, grads, 0.0).astype(BF)
        sl[chunk(8), :] = jnp.where(mask, 0.0, grads).astype(BF)
        for k in range(1, SLOTS - 1):
            weights = s[chunk(k), :] * inverse
            wl[chunk(k), :] = weights.astype(BF)
            sl[chunk(k), :] = (weights * (w[chunk(k), :] - row_dot)).astype(BF)
        acc[0] += jnp.dot(sl[...], qn, preferred_element_type=F32)
        acc[1] += jnp.dot(wl[...], gn, preferred_element_type=F32)
        dqt = jnp.dot(kt[...], sl[...], preferred_element_type=F32) * SCALE
        cols = pl.ds(base, PAIR)
        dq[:, cols] = jnp.concatenate(
            [jnp.transpose(dqt[:, 0:BLOCK]), jnp.transpose(dqt[:, BLOCK:PAIR])], axis=1
        ).astype(BF)

    def collect(h):
        for k in range(SLOTS):
            part[h, k, 0:BLOCK, :] = acc[0, k * BLOCK : (k + 1) * BLOCK, :] * SCALE
            part[h, k, BLOCK : 2 * BLOCK, :] = acc[1, k * BLOCK : (k + 1) * BLOCK, :]

    last = KEY_VALUE_HEADS - 1
    for h in range(KEY_VALUE_HEADS):
        gather_start(h)
    for n, (ref, _) in enumerate(((q, query), (g, out_grad), (o, output))):
        pltpu.make_async_copy(ref, ref, wide_sem.at[n]).wait()
    gather_mid(0)
    gather_forward(0)
    gather_mid(1)
    gather_done(0)

    @pl.loop(0, KEY_VALUE_HEADS)
    def _(h):
        prepare(h)
        pair(h, 0)

        @pl.when(h < last)
        def _():
            gather_forward(h + 1)

        @pl.when(h > 0)
        def _():
            reduce_mid(h - 1)

        pair(h, 1)

        @pl.when(h < last - 1)
        def _():
            gather_mid(h + 2)

        pair(h, 2)

        @pl.when(h > 0)
        def _():
            reduce_column(h - 1)

        pair(h, 3)

        @pl.when(h > 0)
        def _():
            reduce_finish(h - 1)

        collect(h)
        reduce_start(h)
        first = pl.ds(pl.multiple_of(h * GROUP * HEAD_SIZE, GROUP * HEAD_SIZE), GROUP * HEAD_SIZE)
        pltpu.make_async_copy(dq.at[:, first], query_grad.at[:, first], out_sem.at[h]).start()

        @pl.when(h < last)
        def _():
            gather_done(h + 1)

    reduce_mid(last)
    reduce_column(last)
    reduce_finish(last)
    outs = (
        pltpu.make_async_copy(dk, key_gradient, out_sem.at[KEY_VALUE_HEADS]),
        pltpu.make_async_copy(dv, value_gradient, out_sem.at[KEY_VALUE_HEADS + 1]),
    )
    for copy in outs:
        copy.start()
    for h in range(KEY_VALUE_HEADS):
        first = pl.ds(h * GROUP * HEAD_SIZE, GROUP * HEAD_SIZE)
        pltpu.make_async_copy(dq.at[:, first], query_grad.at[:, first], out_sem.at[h]).wait()
    for copy in outs:
        copy.wait()

    @pl.loop(0, KEY_VALUE_HEADS)
    def _(h):
        for slot in range(1, SLOTS):
            gather(h, slot, slot, right).wait_send()
            reduce(h, slot, right).wait_send()


def local(blocks, uly, query, key_input, value_input, output, out_grad):
    tokens = query.shape[0]
    anywhere = pl.BlockSpec(memory_space=pl.ANY)
    heads, slots = KEY_VALUE_HEADS, SLOTS
    rows = QUERY_HEADS * BLOCK
    return pl.pallas_call(
        functools.partial(kernel, blocks, uly),
        out_shape=(
            jax.ShapeDtypeStruct((tokens, QUERY_HEADS * HEAD_SIZE), BF),
            jax.ShapeDtypeStruct((tokens, heads * HEAD_SIZE), BF),
            jax.ShapeDtypeStruct((tokens, heads * HEAD_SIZE), BF),
        ),
        in_specs=[anywhere] * 5,
        out_specs=(anywhere,) * 3,
        scratch_shapes=[
            pltpu.VMEM((rows, HEAD_SIZE), BF),
            pltpu.VMEM((rows, HEAD_SIZE), BF),
            pltpu.VMEM((rows, HEAD_SIZE), BF),
            pltpu.VMEM((heads, slots, 2 * BLOCK, HEAD_SIZE), BF),
            pltpu.VMEM((HEAD_SIZE, SPAN), BF),
            pltpu.VMEM((SPAN, PAIR), F32),
            pltpu.VMEM((SPAN, PAIR), F32),
            pltpu.VMEM((SPAN, PAIR), BF),
            pltpu.VMEM((SPAN, PAIR), BF),
            pltpu.VMEM((2, SPAN, HEAD_SIZE), F32),
            pltpu.VMEM((heads, slots, 2 * BLOCK, HEAD_SIZE), F32),
            pltpu.VMEM((heads, slots, 2 * BLOCK, HEAD_SIZE), BF),
            pltpu.VMEM((heads, slots, 2 * BLOCK, HEAD_SIZE), BF),
            pltpu.VMEM((8, 128), F32),
            pltpu.VMEM((BLOCK, QUERY_HEADS * HEAD_SIZE), BF),
            pltpu.VMEM((BLOCK, heads * HEAD_SIZE), BF),
            pltpu.VMEM((BLOCK, heads * HEAD_SIZE), BF),
            pltpu.SemaphoreType.DMA((heads, 2)),
            pltpu.SemaphoreType.DMA((3,)),
            pltpu.SemaphoreType.DMA((heads, slots)),
            pltpu.SemaphoreType.DMA((heads, slots)),
            pltpu.SemaphoreType.DMA((heads, slots)),
            pltpu.SemaphoreType.DMA((heads, slots)),
            pltpu.SemaphoreType.DMA((heads + 2,)),
        ],
        compiler_params=pltpu.CompilerParams(collective_id=0, has_side_effects=True),
    )(query, key_input, value_input, output, out_grad)


def solution(mesh):
    spec = P(("blk", "uly"), None)
    body = functools.partial(local, mesh.shape["blk"], mesh.shape["uly"])
    return jax.shard_map(
        body, mesh=mesh, in_specs=(spec,) * 5, out_specs=(spec,) * 3, check_vma=False
    )
```

time: 366 us -> 91.9 us (0.25)
  waiting for transfers between devices: 160 us -> 0 us
  matrix products: 93.2 us -> 0 us
  Pallas kernels: 0 us -> 87.1 us
  starting transfers between devices: 57.5 us -> 0 us
  other arithmetic: 26.3 us -> 0 us
  local copies, waits for them, and re-layouts: 24.9 us -> 3.93 us
    all_to_all x8 -> x0, waiting for transfers between devices: 153 us -> none  [the longest x1 28 us: local(): lax.all_to_all(repeat_groups(key_input), 'uly', split_axis=1, concat_axis...]
    dot_general x40 -> x0, matrix products: 93.2 us -> none  [the longest x8 28.2 us: block_step(): jnp.einsum('hqk,qhd->kd', weights_low, grad_block, preferred_element_type...]
    pallas_call x0 -> x1, Pallas kernels: none -> 87.1 us  [local(): pl.pallas_call(functools.partial(kernel, blocks, uly), out_shape=(jax.Sha...]
    all_to_all x8 -> x0, starting transfers between devices: 49.8 us -> none  [the longest x1 11.5 us: local(): lax.all_to_all(repeat_groups(key_input), 'uly', split_axis=1, concat_axis...]
    reduce_sum x11 -> x0, other arithmetic: 18.3 us -> none  [the longest x8 14.2 us: block_step(): jnp.sum(jnp.where(visible, jnp.exp(masked - row_max[:, :, None]), 0.0), a...]
    ppermute x4 -> x0, starting transfers between devices: 7.68 us -> none  [shifted(): lax.ppermute(value, axis, [(source, source + steps) for source in range(l...]
    ppermute x4 -> x0, waiting for transfers between devices: 7.62 us -> none  [shifted(): lax.ppermute(value, axis, [(source, source + steps) for source in range(l...]
    unnamed x10 -> x7, local copies, waits for them, and re-layouts: 10.6 us -> 3.93 us
  transfers between devices with their start and end apart: 12 -> 0, of which waited for: 10 -> 0; matrix products, arithmetic and copies ran while one was open for 7% -> 0% of each run, Pallas kernels for 0% -> 0%
where the time goes in v1:
time: 91.9 us; the launch traced here: 91.6 us
  Pallas kernels  87.1 us (95%)
  local copies, waits for them, and re-layouts  3.93 us (4%)
    pallas_call x1, Pallas kernels, local(): pl.pallas_call(functools.partial(kernel, blocks, uly), out_shape=(jax.Sha...  87.1 us
    unnamed x7, local copies, waits for them, and re-layouts  3.93 us

profile of v1, /device:TPU:6, one launch (start us, length us, event | category | flops | bytes accessed | tf_op | source)
XLA Modules:
  0.0 91.6 jit_solution(6768914103751733979)
XLA Ops:
  0.6 87.1 %shard_map.76 = (bf16[128,4096]{1,0:T(8,128)(2,1)}, bf16[128,512]{1,0:T(8,128)(2,1)}, bf16[128,512]{1,0:T(8,128)(2,1)}) custom-call(bf16[128,4096]{1,0:T(8,128)(2,1)} %query.1, bf16[128,512]{1,0:T(8,128)(2,1)} %key.1, bf16[128,512]{1,0:T(8,128)(2,1)} %value.1, bf16[128,4096]{1,0:T(8,128)(2,1)} %output.1, bf16[128,4096]{1,0:T(8,128)(2,1)} %out_grad.1), custom_call_target="tpu_custom_call" | custom-call | tf_op jit(solution)/shard_map/pallas_call | solution.py:322
  87.7 0.0 copy-start.1
  87.7 2.3 %copy.11 = bf16[128,4096]{1,0:T(8,128)(2,1)} copy(bf16[128,4096]{1,0:T(8,128)(2,1)} %get-tuple-element.6) | data formatting | bytes 2097152
  90.0 0.0 copy-done.1
  90.0 0.0 copy-start
  90.0 0.7 copy.12
  90.7 0.3 copy-done
  91.0 0.7 copy.13
Async XLA Ops:
  87.7 2.3 %copy-start.1 = (bf16[128,512]{1,0:T(8,128)(2,1)S(1)}, bf16[128,512]{1,0:T(8,128)(2,1)}, u32[]{:S(2)}) copy-start(bf16[128,512]{1,0:T(8,128)(2,1)} %get-tuple-element.7) | copy-start | bytes 393220
  90.0 1.0 %copy-start = (bf16[128,512]{1,0:T(8,128)(2,1)S(1)}, bf16[128,512]{1,0:T(8,128)(2,1)}, u32[]{:S(2)}) copy-start(bf16[128,512]{1,0:T(8,128)(2,1)} %get-tuple-element.8) | copy-start | bytes 393220

commit v2 on v1

v2 whole, which is shorter than its diff:
```python
import functools

import jax
import jax.numpy as jnp
from jax import lax
from jax.experimental import pallas as pl
from jax.experimental.pallas import tpu as pltpu
from jax.sharding import PartitionSpec as P

QUERY_HEADS = 32
KEY_VALUE_HEADS = 4
HEAD_SIZE = 128
WINDOW_KEYS = 1024
ROW = 4
GROUP = QUERY_HEADS // KEY_VALUE_HEADS
BLOCK = 128
SLOTS = WINDOW_KEYS // BLOCK + 1
PAIR = 2 * BLOCK
STEPS = GROUP // 2
SPAN = SLOTS * BLOCK
SCALE = HEAD_SIZE**-0.5
LOG2E = 1.4426950408889634
BIG = 1e30
BF, F32 = jnp.bfloat16, jnp.float32
NT = (((1,), (1,)), ((), ()))
MESH = pl.DeviceIdType.MESH


ITEMS = 2 * KEY_VALUE_HEADS
CUTS = 4
PARTS = 2
ROWS = GROUP * BLOCK


def kernel(
    blocks, uly,
    query, key, value, output, out_grad,
    query_grad, key_gradient, value_gradient,
    q, o, g, kv, kt, s, w, wl, sl, rd, ak, av, part, send, land, dq, dk, dv,
    load_sem, wide_sem, gs, gr, rs, rr, out_sem,
):
    blk, u = lax.axis_index("blk"), lax.axis_index("uly")
    z_count = uly // ROW
    y, z = u % ROW, u // ROW
    device = blk * uly + u
    row = blk * z_count + z
    rows = blocks * z_count
    at_end = (y + 1) // ROW
    at_start = 1 - (y + ROW - 1) // ROW

    def along_y(step):
        return (blk, z * ROW + (y + step + ROW) % ROW)

    def along_z(step):
        to = (row + step + rows) % rows
        return (to // z_count, (to % z_count) * ROW + y)

    right, left, up, down = along_y(1), along_y(-1), along_z(1), along_z(-1)

    barrier = pltpu.get_barrier_semaphore()
    for other in (right, left, up, down):
        pl.semaphore_signal(barrier, inc=1, device_id=other, device_id_type=MESH)

    def load_kv(item):
        cols = pl.ds(item // 2 * HEAD_SIZE, HEAD_SIZE)
        source = value if item % 2 else key
        return pltpu.make_async_copy(source.at[:, cols], kv.at[item, 0], load_sem.at[item])

    for item in range(ITEMS):
        load_kv(item).start()

    @pl.loop(0, QUERY_HEADS)
    def _(n):
        cols = pl.ds(pl.multiple_of(n * HEAD_SIZE, HEAD_SIZE), HEAD_SIZE)
        here = pl.ds(pl.multiple_of(n * BLOCK, BLOCK), BLOCK)
        pltpu.make_async_copy(out_grad.at[:, cols], g.at[here, :], wide_sem.at[1]).start()
        pltpu.make_async_copy(output.at[:, cols], o.at[here, :], wide_sem.at[2]).start()
        pltpu.make_async_copy(query.at[:, cols], q.at[here, :], wide_sem.at[0]).start()

    for item in range(ITEMS):
        load_kv(item).wait()
    pl.semaphore_wait(barrier, 4)

    def gather(item, source, to, other):
        return pltpu.make_async_remote_copy(
            src_ref=kv.at[item, source], dst_ref=kv.at[item, to],
            send_sem=gs.at[item, to], recv_sem=gr.at[item, to],
            device_id=other, device_id_type=MESH,
        )

    def arrived(item, slot):
        gather(item, slot, slot, right).wait_recv()

    def gather_start(item):
        gather(item, 0, 4, up).start()

        @pl.when(y < ROW - 1)
        def _():
            gather(item, 0, 1, right).start()

        @pl.when(y == 0)
        def _():
            gather(item, 0, 3, left).start()

    def gather_four(item):
        arrived(item, 4)
        gather(item, 4, 8, up).start()
        gather(item, 4, 5 - 4 * at_end, right).start()
        gather(item, 4, 3 + 4 * at_start, left).start()

    def gather_eight(item):
        arrived(item, 8)

        @pl.when(y == ROW - 1)
        def _():
            gather(item, 8, 5, right).start()

        @pl.when(y > 0)
        def _():
            gather(item, 8, 7, left).start()

    def gather_forward(item):
        arrived(item, 1)
        arrived(item, 5)
        gather(item, 1 + 4 * at_end, 2, right).start()
        arrived(item, 3)
        arrived(item, 7)
        gather(item, 7 - 4 * at_start, 6, left).start()

    def gather_done(item):
        arrived(item, 2)
        arrived(item, 6)

    def reduce(item, slot, other):
        return pltpu.make_async_remote_copy(
            src_ref=send.at[item, slot], dst_ref=land.at[item, slot],
            send_sem=rs.at[item, slot], recv_sem=rr.at[item, slot],
            device_id=other, device_id_type=MESH,
        )

    def slot_rows(slot):
        if isinstance(slot, int):
            return pl.ds(slot * BLOCK, BLOCK)
        return pl.ds(pl.multiple_of(slot * BLOCK, BLOCK), BLOCK)

    def ready(item, slot):
        send[item, slot] = part[item, slot_rows(slot), :].astype(BF)

    def take(item, slot, into):
        reduce(item, slot, right).wait_recv()
        here = slot_rows(into)
        part[item, here, :] = part[item, here, :] + land[item, slot].astype(F32)

    def reduce_start(item):
        for slot in (2, 6, 5 - 4 * at_end, 3 + 4 * at_start):
            ready(item, slot)
        reduce(item, 2, left).start()
        reduce(item, 6, right).start()
        reduce(item, 5 - 4 * at_end, left).start()
        reduce(item, 3 + 4 * at_start, right).start()

    def reduce_mid(item):
        take(item, 2, 1 + 4 * at_end)
        ready(item, 1 + 4 * at_end)
        take(item, 6, 7 - 4 * at_start)
        ready(item, 7 - 4 * at_start)
        reduce(item, 1 + 4 * at_end, left).start()
        reduce(item, 7 - 4 * at_start, right).start()

    def reduce_column(item):
        take(item, 5, 4 + 4 * at_end)
        take(item, 7, 8 - 4 * at_start)
        ready(item, 8)
        take(item, 1, 4 * at_end)
        take(item, 3, 4 - 4 * at_start)
        reduce(item, 8, down).start()

    def reduce_eight(item):
        take(item, 8, 4)
        ready(item, 4)
        reduce(item, 4, down).start()

    def reduce_finish(item):
        take(item, 4, 0)

        to = dk if item % 2 else dv
        to[:, pl.ds(item // 2 * HEAD_SIZE, HEAD_SIZE)] = part[item, 0:BLOCK, :].astype(BF)

    lane = lax.broadcasted_iota(jnp.int32, (BLOCK, PAIR), 1) % BLOCK
    mask = lax.broadcasted_iota(jnp.int32, (BLOCK, PAIR), 0) <= lane

    def chunk(k):
        return pl.ds(k * BLOCK, BLOCK)

    def pair_rows(h, n):
        return pl.ds(pl.multiple_of((h * STEPS + n) * PAIR, PAIR), PAIR)

    def hidden(k):
        return jnp.where(device >= k, 0.0, BIG).astype(F32)

    def row_dots(index):
        at = pl.ds(pl.multiple_of(index * PAIR, PAIR), PAIR)
        product = o[at, :].astype(F32) * g[at, :].astype(F32)
        high = product.astype(BF)
        low = (product - high.astype(F32)).astype(BF)
        ones = jnp.ones((8, HEAD_SIZE), BF)
        rd[index] = lax.dot_general(ones, high, NT, preferred_element_type=F32) + lax.dot_general(
            ones, low, NT, preferred_element_type=F32
        )

    def keys_of(h):
        return kv[2 * h].reshape(SPAN, HEAD_SIZE)

    def values_of(h):
        return kv[2 * h + 1].reshape(SPAN, HEAD_SIZE)

    def scores(h, n):
        s[...] = lax.dot_general(keys_of(h), q[pair_rows(h, n), :], NT, preferred_element_type=F32)

    def products(h, n):
        w[...] = lax.dot_general(values_of(h), g[pair_rows(h, n), :], NT, preferred_element_type=F32)

    def soft(n):
        cols = pl.ds(n * PAIR, PAIR)
        edge = jnp.where(mask, s[chunk(0), :], s[chunk(8), :] - hidden(8))
        s[chunk(0), :] = edge
        top = jnp.max(edge, axis=0, keepdims=True)
        for k in range(1, SLOTS - 1):
            top = jnp.maximum(top, jnp.max(s[chunk(k), :], axis=0, keepdims=True) - hidden(k))
        factor = SCALE * LOG2E
        total = jnp.zeros((1, PAIR), F32)
        for k in range(SLOTS - 1):
            p = jnp.exp2((s[chunk(k), :] - (top + hidden(k))) * factor)
            s[chunk(k), :] = p
            total = total + jnp.sum(p, axis=0, keepdims=True)
        inverse = 1.0 / total
        weights = s[chunk(0), :] * inverse
        wl[chunk(0), cols] = jnp.where(mask, weights, 0.0).astype(BF)
        wl[chunk(8), cols] = jnp.where(mask, 0.0, weights).astype(BF)
        for k in range(1, SLOTS - 1):
            wl[chunk(k), cols] = (s[chunk(k), :] * inverse).astype(BF)

    def grad(h, n):
        cols = pl.ds(n * PAIR, PAIR)
        row_dot = rd[h * STEPS + n, 0:1, :]
        for k in range(SLOTS):
            sl[chunk(k), cols] = (wl[chunk(k), cols].astype(F32) * (w[chunk(k), :] - row_dot)).astype(BF)

    def query_side(h, n):
        cols = pl.ds(n * PAIR, PAIR)
        dqt = jnp.dot(kt[...], sl[:, cols], preferred_element_type=F32) * SCALE
        dq[:, pair_rows(h, n)] = jnp.concatenate(
            [jnp.transpose(dqt[:, 0:BLOCK]), jnp.transpose(dqt[:, BLOCK:PAIR])], axis=1
        ).astype(BF)

    def add_keys(h, n):
        term = jnp.dot(sl[:, pl.ds(n * PAIR, PAIR)], q[pair_rows(h, n), :], preferred_element_type=F32)
        ak[...] = term if n == 0 else ak[...] + term

    def add_values(h, n):
        term = jnp.dot(wl[:, pl.ds(n * PAIR, PAIR)], g[pair_rows(h, n), :], preferred_element_type=F32)
        av[...] = term if n == 0 else av[...] + term

    def turn(h):
        for k in range(SLOTS):
            kt[:, k * BLOCK : (k + 1) * BLOCK] = jnp.transpose(kv[2 * h, k])

    def all_row_dots(_):
        for n, ref in ((2, o), (1, g)):
            pltpu.make_async_copy(ref, ref, wide_sem.at[n]).wait()

        @pl.loop(0, QUERY_HEADS // 2)
        def _(index):
            row_dots(index)

        pltpu.make_async_copy(q, q, wide_sem.at[0]).wait()

    def write_queries(h):
        cols = pl.ds(h * GROUP * HEAD_SIZE, GROUP * HEAD_SIZE)
        return pltpu.make_async_copy(dq.at[:, cols], query_grad.at[:, cols], out_sem.at[h])

    def stage_part(index):
        t = index // PARTS
        width = STEPS // PARTS
        first = index % PARTS * width
        if t > 0 and first == 0:
            turn(t - 1)
        for n in range(first, first + width):
            if t > 0:
                products(t - 1, n)
            if t < KEY_VALUE_HEADS:
                scores(t, n)
            if t > 0:
                grad(t - 1, n)
            if t < KEY_VALUE_HEADS and n > 0:
                add_values(t, n - 1)
            if t > 0:
                query_side(t - 1, n)
                add_keys(t - 1, n)
            if t < KEY_VALUE_HEADS:
                soft(n)

    def stage_end(t):
        if t < KEY_VALUE_HEADS:
            add_values(t, STEPS - 1)
            part[2 * t] = av[...]
        if t > 0:
            part[2 * t - 1] = ak[...] * SCALE
            write_queries(t - 1).start()

    plan = (
        (gather_start, 0), (gather_start, 1), (gather_start, 2), (gather_start, 4),
        (gather_four, 0), (gather_four, 1), (gather_four, 2), (gather_eight, 0), (gather_start, 3),
        (gather_four, 4), (gather_eight, 2), (gather_start, 6), (gather_eight, 1),
        (gather_start, 5), (gather_forward, 0), (gather_four, 3), (gather_start, 7),
        (all_row_dots, 0), (gather_forward, 2), (gather_eight, 4), (gather_eight, 3),
        (gather_forward, 1), (gather_four, 5), (gather_done, 0), (gather_four, 6), (stage_part, 0),
        (stage_part, 1), (gather_forward, 4), (gather_eight, 6), (stage_end, 0), (gather_done, 1),
        (gather_eight, 5), (gather_forward, 3), (reduce_start, 0), (gather_four, 7),
        (gather_done, 2), (stage_part, 2), (stage_part, 3), (gather_eight, 7), (stage_end, 1),
        (reduce_start, 1), (gather_forward, 5), (gather_forward, 6), (gather_done, 4),
        (reduce_start, 2), (gather_done, 3), (stage_part, 4), (reduce_mid, 0), (stage_part, 5),
        (gather_forward, 7), (stage_end, 2), (reduce_mid, 1), (reduce_start, 3), (gather_done, 5),
        (reduce_start, 4), (gather_done, 6), (stage_part, 6), (reduce_mid, 2), (stage_part, 7),
        (reduce_mid, 3), (stage_end, 3), (reduce_start, 5), (reduce_column, 0), (gather_done, 7),
        (reduce_column, 1), (reduce_start, 6), (stage_part, 8), (reduce_mid, 4), (stage_part, 9),
        (reduce_column, 2), (reduce_eight, 0), (stage_end, 4), (reduce_start, 7),
        (reduce_eight, 1), (reduce_mid, 6), (reduce_mid, 5), (reduce_column, 3),
        (reduce_finish, 0), (reduce_column, 4), (reduce_eight, 2), (reduce_mid, 7),
        (reduce_eight, 3), (reduce_column, 6), (reduce_column, 5), (reduce_finish, 1),
        (reduce_eight, 4), (reduce_column, 7), (reduce_eight, 5), (reduce_finish, 3),
        (reduce_finish, 2), (reduce_eight, 6), (reduce_eight, 7), (reduce_finish, 6),
        (reduce_finish, 5), (reduce_finish, 4), (reduce_finish, 7),
    )
    for act, index in plan:
        act(index)
    narrow = (
        pltpu.make_async_copy(dk, key_gradient, out_sem.at[KEY_VALUE_HEADS]),
        pltpu.make_async_copy(dv, value_gradient, out_sem.at[KEY_VALUE_HEADS + 1]),
    )
    for copy in narrow:
        copy.start()
    for copy in (*narrow, *(write_queries(h) for h in range(KEY_VALUE_HEADS))):
        copy.wait()

    @pl.loop(0, ITEMS)
    def _(item):
        for slot in range(1, SLOTS):
            gather(item, slot, slot, right).wait_send()
            reduce(item, slot, right).wait_send()


def hand_over(wide, narrow_1, narrow_2, out, out_1, out_2, held, held_1, held_2, sems):
    width = wide.shape[1] // CUTS
    cuts = [pl.ds(n * width, width) for n in range(CUTS)]
    moves = [(wide.at[:, c], held.at[:, c], out.at[:, c]) for c in cuts]
    moves += [(narrow_1, held_1, out_1), (narrow_2, held_2, out_2)]
    reads = [pltpu.make_async_copy(a, b, sems.at[0, n]) for n, (a, b, _) in enumerate(moves)]
    writes = [pltpu.make_async_copy(b, c, sems.at[1, n]) for n, (_, b, c) in enumerate(moves)]
    for read in reads:
        read.start()
    for read, write in zip(reads, writes):
        read.wait()
        write.start()
    for write in writes:
        write.wait()


def publish(outs, results):
    anywhere = pl.BlockSpec(memory_space=pl.ANY)
    return pl.pallas_call(
        hand_over,
        out_shape=outs,
        in_specs=[anywhere] * 3,
        out_specs=(anywhere,) * 3,
        scratch_shapes=[
            *(pltpu.VMEM(out.shape, BF) for out in outs),
            pltpu.SemaphoreType.DMA((2, CUTS + 2)),
        ],
    )(*results)


def local(blocks, uly, query, key_input, value_input, output, out_grad):
    tokens = query.shape[0]
    anywhere = pl.BlockSpec(memory_space=pl.ANY)
    rows = QUERY_HEADS * BLOCK
    outs = (
        jax.ShapeDtypeStruct((tokens, QUERY_HEADS * HEAD_SIZE), BF),
        jax.ShapeDtypeStruct((tokens, KEY_VALUE_HEADS * HEAD_SIZE), BF),
        jax.ShapeDtypeStruct((tokens, KEY_VALUE_HEADS * HEAD_SIZE), BF),
    )
    results = pl.pallas_call(
        functools.partial(kernel, blocks, uly),
        out_shape=outs,
        in_specs=[anywhere] * 5,
        out_specs=(anywhere,) * 3,
        scratch_shapes=[
            pltpu.VMEM((rows, HEAD_SIZE), BF),
            pltpu.VMEM((rows, HEAD_SIZE), BF),
            pltpu.VMEM((rows, HEAD_SIZE), BF),
            pltpu.VMEM((ITEMS, SLOTS, BLOCK, HEAD_SIZE), BF),
            pltpu.VMEM((HEAD_SIZE, SPAN), BF),
            pltpu.VMEM((SPAN, PAIR), F32),
            pltpu.VMEM((SPAN, PAIR), F32),
            pltpu.VMEM((SPAN, ROWS), BF),
            pltpu.VMEM((SPAN, ROWS), BF),
            pltpu.VMEM((QUERY_HEADS // 2, 8, PAIR), F32),
            pltpu.VMEM((SPAN, HEAD_SIZE), F32),
            pltpu.VMEM((SPAN, HEAD_SIZE), F32),
            pltpu.VMEM((ITEMS, SPAN, HEAD_SIZE), F32),
            pltpu.VMEM((ITEMS, SLOTS, BLOCK, HEAD_SIZE), BF),
            pltpu.VMEM((ITEMS, SLOTS, BLOCK, HEAD_SIZE), BF),
            *(pltpu.VMEM(out.shape, BF) for out in outs),
            pltpu.SemaphoreType.DMA((ITEMS,)),
            pltpu.SemaphoreType.DMA((3,)),
            pltpu.SemaphoreType.DMA((ITEMS, SLOTS)),
            pltpu.SemaphoreType.DMA((ITEMS, SLOTS)),
            pltpu.SemaphoreType.DMA((ITEMS, SLOTS)),
            pltpu.SemaphoreType.DMA((ITEMS, SLOTS)),
            pltpu.SemaphoreType.DMA((KEY_VALUE_HEADS + 2,)),
        ],
        compiler_params=pltpu.CompilerParams(collective_id=0, has_side_effects=True),
    )(query, key_input, value_input, output, out_grad)
    return publish(outs, results)


def solution(mesh):
    spec = P(("blk", "uly"), None)
    body = functools.partial(local, mesh.shape["blk"], mesh.shape["uly"])
    return jax.shard_map(
        body, mesh=mesh, in_specs=(spec,) * 5, out_specs=(spec,) * 3, check_vma=False
    )
```

time: 91.9 us -> 63.5 us (0.69)
  Pallas kernels: 87.1 us -> 62.5 us
  local copies, waits for them, and re-layouts: 3.93 us -> 0 us
    pallas_call x1 -> x2, Pallas kernels: 87.1 us -> 62.5 us  [the longest x1 60.4 us: local(): pl.pallas_call(functools.partial(kernel, blocks, uly), out_shape=outs, in...]
    unnamed x7 -> x0, local copies, waits for them, and re-layouts: 3.93 us -> none
where the time goes in v2:
time: 63.5 us; the launch traced here: 63.3 us
  Pallas kernels  62.5 us (98%)
  between operations  0.8 us (1%)
    pallas_call x1, Pallas kernels, local(): pl.pallas_call(functools.partial(kernel, blocks, uly), out_shape=outs, in...  60.4 us
    pallas_call x1, Pallas kernels, publish(): pl.pallas_call(hand_over, out_shape=outs, in_specs=[anywhere] * 3, out_sp...  2.1 us

profile of v2, /device:TPU:6, one launch (start us, length us, event | category | flops | bytes accessed | tf_op | source)
XLA Modules:
  0.0 63.3 jit_solution(17345544998101059708)
XLA Ops:
  0.6 60.4 %shard_map.76 = (bf16[128,4096]{1,0:T(8,128)(2,1)}, bf16[128,512]{1,0:T(8,128)(2,1)}, bf16[128,512]{1,0:T(8,128)(2,1)}) custom-call(bf16[128,4096]{1,0:T(8,128)(2,1)} %query.1, bf16[128,512]{1,0:T(8,128)(2,1)} %key.1, bf16[128,512]{1,0:T(8,128)(2,1)} %value.1, bf16[128,4096]{1,0:T(8,128)(2,1)} %output.1, bf16[128,4096]{1,0:T(8,128)(2,1)} %out_grad.1), custom_call_target="tpu_custom_call" | custom-call | tf_op jit(solution)/shard_map/pallas_call | solution.py:392
  61.1 2.1 %shard_map.77 = (bf16[128,4096]{1,0:T(8,128)(2,1)}, bf16[128,512]{1,0:T(8,128)(2,1)}, bf16[128,512]{1,0:T(8,128)(2,1)}) custom-call(bf16[128,4096]{1,0:T(8,128)(2,1)} %get-tuple-element.6.wide, bf16[128,512]{1,0:T(8,128)(2,1)} %get-tuple-element.7.narrow_1, bf16[128,512]{1,0:T(8,128)(2,1)} %get-tuple-element.8.narrow_2), custom_call_target="tpu_custom_call" | custom-call | tf_op jit(solution)/shard_map/pallas_call | solution.py:371
